TPU v7x, 128 devices: a whole 4x4x4 slice. The times are simulated.
128 devices in a mesh: src: 16 (over y, z), reg: 8 (over x, core).
Axes of the slice: x: 4, y: 4, z: 4, core: 2. Of those that a mesh axis runs over, the one named last changes fastest.
Arguments:
- tiles: bfloat16 [65536, 128, 128], P(('src', 'reg')), may hold values from -0.1875 to 0.1875
- rays: float32 [8192, 128], P(('src', 'reg')), may hold values from -6 to 6
- tile_rows: int32 [65536], P(('src', 'reg')), may hold values from 0 to 63, as said below
- tile_slots: int32 [65536], P(('src', 'reg')), may hold values from 0 to 255, as said below
- tile_count: int32 [128], P(('src', 'reg')), may hold values from 256 to 512, as said below
- wanted: int32 [128, 128, 2], P(('src', 'reg')), may hold values from 0 to 255
Outputs:
- solution: float32 [32768, 128], P(('src', 'reg'))
- right_vector: float32 [32768, 128], P(('src', 'reg'))
Inputs may be any that keep to these rules, and one draw needn't show every extreme that they name: `tile_rows`: non-decreasing along each device's 512 tiles. `tile_slots`: the first 256 tiles of each device name every slot once. `tile_count`: some device has all 512 tiles live.
All inputs are finite; a program needn't handle non-finite values.
Results may differ from a plain program's by a relative error of at most 0.024.
Values may be sent and summed in bfloat16 or wider, within the bound.
No kernel may reach another device: no remote copies, remote signals or barrier semaphores. Data moves between devices by JAX's collectives and lax.ppermute only.
A program may use at most 128 MiB of HBM per device.

v0:
```python
import jax
import jax.numpy as jnp
from jax import lax
from jax.sharding import Mesh
from jax.sharding import PartitionSpec as P

BLK_DEV = 256
ITERS = 3
SRC_REG = ("src_0", "src_1", "reg_0", "reg_1")


damping = 0.5


def over_axes(value, axes):
    for axis in axes:
        value = lax.psum(value, axis)
    return value


def per_device(tiles, rays, tile_rows, tile_slots, tile_count, wanted):
    device_list = lax.axis_size(SRC_REG)
    width = tiles.shape[2]
    row_blocks = rays.shape[0]
    cap = wanted.shape[2]
    requests = wanted[0].reshape(-1)
    live = (jnp.arange(tiles.shape[0], dtype=jnp.int32) < tile_count[0]).astype(jnp.float32)[
        :, None
    ]
    u = jnp.zeros_like(rays)
    v = jnp.zeros((BLK_DEV, width), jnp.float32)
    solution = jnp.zeros((BLK_DEV, width), jnp.float32)
    w = jnp.zeros((BLK_DEV, width), jnp.float32)
    uraw = rays
    vraw = v
    alpha = jnp.float32(1.0)
    phibar = jnp.float32(0.0)
    rhobar = jnp.float32(0.0)
    for step in range(ITERS + 1):
        if step > 0:
            outgoing = vraw.astype(jnp.bfloat16)[requests].reshape(device_list, cap, width)
            incoming = lax.all_to_all(outgoing, SRC_REG, split_axis=0, concat_axis=0, tiled=True)
            fetched = incoming.reshape(device_list * cap, width)
            forward_picked = fetched[tile_slots]
            product = (
                jnp.einsum("tij,tj->ti", tiles, forward_picked, preferred_element_type=jnp.float32)
                * live
            )
            uraw = (
                jax.ops.segment_sum(product, tile_rows, num_segments=row_blocks) / alpha - alpha * u
            )
        picked = uraw.astype(jnp.bfloat16)[tile_rows]
        contrib = jnp.einsum("tij,ti->tj", tiles, picked, preferred_element_type=jnp.float32) * live
        adjoint_slot_sums = jax.ops.segment_sum(contrib, tile_slots, num_segments=device_list * cap)
        slot_sums = adjoint_slot_sums.reshape(device_list, cap, width)
        returned = lax.all_to_all(
            slot_sums.astype(jnp.bfloat16), SRC_REG, split_axis=0, concat_axis=0, tiled=True
        ).astype(slot_sums.dtype)
        adjoint_returned = returned.reshape(device_list * cap, width)
        grad = jax.ops.segment_sum(adjoint_returned, requests, num_segments=BLK_DEV)
        sum_uu, sum_pp, sum_pv, sum_vv = (
            over_axes(jnp.sum(uraw * uraw), SRC_REG),
            over_axes(jnp.sum(grad * grad), SRC_REG),
            over_axes(jnp.sum(grad * v), SRC_REG),
            over_axes(jnp.sum(v * v), SRC_REG),
        )
        beta = jnp.sqrt(sum_uu)
        vraw = grad / beta - beta * v
        alpha_new = jnp.sqrt(sum_pp / sum_uu - 2.0 * sum_pv + sum_uu * sum_vv)
        u = uraw / beta
        v_new = vraw / alpha_new
        if step == 0:
            w = v_new
            phibar = beta
            rhobar = alpha_new
        else:
            rhobar1 = jnp.sqrt(rhobar * rhobar + damping * damping)
            phibar = rhobar / rhobar1 * phibar
            rho = jnp.sqrt(rhobar1 * rhobar1 + beta * beta)
            cosine = rhobar1 / rho
            sine = beta / rho
            theta = sine * alpha_new
            rhobar = -cosine * alpha_new
            phi = cosine * phibar
            phibar = sine * phibar
            solution = solution + phi / rho * w
            w = v_new - theta / rho * w
        v = v_new
        alpha = alpha_new
    scale = jnp.sqrt(jnp.float32(BLK_DEV * width * device_list))
    return (solution, v * scale)


def solution(mesh):
    split = Mesh(mesh.devices.reshape(4, 4, 4, 2), ("src_0", "src_1", "reg_0", "reg_1"))
    placed = (
        P(SRC_REG, None, None),
        P(SRC_REG, None),
        P(SRC_REG),
        P(SRC_REG),
        P(SRC_REG),
        P(SRC_REG, None, None),
    )
    return jax.shard_map(
        per_device,
        mesh=split,
        in_specs=placed,
        out_specs=(P(SRC_REG, None), P(SRC_REG, None)),
        check_vma=False,
    )
```

profile of v0, /device:TPU:1, one launch (start us, length us, event | category | flops | bytes accessed | tf_op | source)
XLA Modules:
  0.0 359.4 jit_solution(1995274523629218105)
XLA Ops:
  4.8 8.1 %fusion.12 = f32[512,1,128]{2,1,0:T(1,128)S(1)} fusion(bf16[512,128,128]{2,1,0:T(8,128)(2,1)} %param.6, bf16[512,128,1]{1,0,2:T(8,128)(2,1)S(1)} %bitcast.59), kind=kOutput, calls=%fused_computation.33 | convolution fusion | flops 16777216 | bytes 17170432 | tf_op jit(solution)/shard_map/tij,ti->tj/dot_general | solution.py:53
  15.9 11.5 %all-to-all-start = ((bf16[128,2,128]{2,1,0:T(2,128)(2,1)}), bf16[128,2,128]{2,1,0:T(2,128)(2,1)S(1)}, u32[]{:S(2)}, u32[]{:S(2)}) async-start(bf16[128,2,128]{2,1,0:T(2,128)(2,1)} %bitcast.4), calls=%async_computation | async-start | bytes 131072 | tf_op jit(solution)/shard_map/all_to_all | solution.py:56
  27.9 9.0 %all-to-all-done = bf16[128,2,128]{2,1,0:T(2,128)(2,1)S(1)} async-done(((bf16[128,2,128]{2,1,0:T(2,128)(2,1)}), bf16[128,2,128]{2,1,0:T(2,128)(2,1)S(1)}, u32[]{:S(2)}, u32[]{:S(2)}) %all-to-all-start) | async-done | bytes 65568 | tf_op jit(solution)/shard_map/all_to_all | solution.py:56
  39.0 8.0 %all-reduce.11 = (f32[]{:T(128)}, f32[]{:T(128)}, f32[]{:T(128)}, f32[]{:T(128)}) all-reduce(f32[]{:T(128)} %get-tuple-element.12, f32[]{:T(128)} %get-tuple-element.87, f32[]{:T(128)} %get-tuple-element.11, f32[]{:T(128)} %constant.7.clone.1), channel_id=1, replica_groups=mesh['src_0'=4,'src_1'=4,'reg_0'=4,'reg_1'=2] {'src_0'}, use_global_device_ids=true, to_apply=%region_3.0 | all-reduce | flops 4 | bytes 32 | tf_op jit(solution)/shard_map/psum | solution.py:17
  54.5 7.6 %all-reduce.3 = (f32[]{:T(128)}, f32[]{:T(128)}, f32[]{:T(128)}, f32[]{:T(128)}) all-reduce(f32[]{:T(128)} %get-tuple-element.41, f32[]{:T(128)} %get-tuple-element.42, f32[]{:T(128)} %get-tuple-element.43, f32[]{:T(128)} %get-tuple-element.44), channel_id=1, replica_groups=mesh['src_0'=4,'src_1'=4,'reg_0'=4,'reg_1'=2] {'reg_0'}, use_global_device_ids=true, to_apply=%region_5.0 | all-reduce | flops 4 | bytes 32 | tf_op jit(solution)/shard_map/psum | solution.py:17
  62.1 9.5 %all-reduce.15 = (f32[]{:T(128)}, f32[]{:T(128)}, f32[]{:T(128)}, f32[]{:T(128)}) all-reduce(f32[]{:T(128)} %get-tuple-element.25, f32[]{:T(128)} %get-tuple-element.26, f32[]{:T(128)} %get-tuple-element.27, f32[]{:T(128)} %get-tuple-element.28), channel_id=1, replica_groups=mesh['src_0'=4,'src_1'=4,'reg_0'=4,'reg_1'=2] {'reg_1'}, use_global_device_ids=true, to_apply=%region_6.0 | all-reduce | flops 4 | bytes 32 | tf_op jit(solution)/shard_map/psum | solution.py:17
  88.7 12.2 %fusion.10 = f32[512,1,128]{2,1,0:T(1,128)S(1)} fusion(bf16[512,128,128]{2,1,0:T(8,128)(2,1)} %param.6, bf16[512,128,1]{1,0,2:T(8,128)(2,1)S(1)} %bitcast.53), kind=kOutput, calls=%fused_computation.31 | convolution fusion | flops 16777216 | bytes 17170432 | tf_op jit(solution)/shard_map/tij,tj->ti/dot_general | solution.py:46
  107.0 8.1 %fusion.8 = f32[512,1,128]{2,1,0:T(1,128)S(1)} fusion(bf16[512,128,128]{2,1,0:T(8,128)(2,1)} %param.6, bf16[512,128,1]{1,0,2:T(8,128)(2,1)S(1)} %bitcast.60), kind=kOutput, calls=%fused_computation.29 | convolution fusion | flops 16777216 | bytes 17170432 | tf_op jit(solution)/shard_map/tij,ti->tj/dot_general | solution.py:53
  117.5 13.9 %all_to_all.35 = bf16[128,2,128]{2,1,0:T(2,128)(2,1)S(1)} all-to-all(bf16[128,2,128]{2,1,0:T(2,128)(2,1)S(1)} %bitcast.68), channel_id=1, replica_groups=mesh['src_0'=4,'src_1'=4,'reg_0'=4,'reg_1'=2] {'src_0','src_1','reg_0','..., dimensions={0} | all-to-all | bytes 131072 | tf_op jit(solution)/shard_map/all_to_all | solution.py:56
  133.7 7.5 %all-reduce.10 = (f32[]{:T(128)}, f32[]{:T(128)}, f32[]{:T(128)}, f32[]{:T(128)}) all-reduce(f32[]{:T(128)} %get-tuple-element.10, f32[]{:T(128)} %get-tuple-element.83, f32[]{:T(128)} %get-tuple-element.9, f32[]{:T(128)} %get-tuple-element.8), channel_id=1, replica_groups=mesh['src_0'=4,'src_1'=4,'reg_0'=4,'reg_1'=2] {'src_0'}, use_global_device_ids=true, to_apply=%region_30.0 | all-reduce | flops 4 | bytes 32 | tf_op jit(solution)/shard_map/psum | solution.py:17
  148.6 7.6 %all-reduce.2 = (f32[]{:T(128)}, f32[]{:T(128)}, f32[]{:T(128)}, f32[]{:T(128)}) all-reduce(f32[]{:T(128)} %get-tuple-element.37, f32[]{:T(128)} %get-tuple-element.38, f32[]{:T(128)} %get-tuple-element.39, f32[]{:T(128)} %get-tuple-element.40), channel_id=1, replica_groups=mesh['src_0'=4,'src_1'=4,'reg_0'=4,'reg_1'=2] {'reg_0'}, use_global_device_ids=true, to_apply=%region_32.0 | all-reduce | flops 4 | bytes 32 | tf_op jit(solution)/shard_map/psum | solution.py:17
  156.2 9.5 %all-reduce.14 = (f32[]{:T(128)}, f32[]{:T(128)}, f32[]{:T(128)}, f32[]{:T(128)}) all-reduce(f32[]{:T(128)} %get-tuple-element.21, f32[]{:T(128)} %get-tuple-element.22, f32[]{:T(128)} %get-tuple-element.23, f32[]{:T(128)} %get-tuple-element.24), channel_id=1, replica_groups=mesh['src_0'=4,'src_1'=4,'reg_0'=4,'reg_1'=2] {'reg_1'}, use_global_device_ids=true, to_apply=%region_33.0 | all-reduce | flops 4 | bytes 32 | tf_op jit(solution)/shard_map/psum | solution.py:17
  182.8 12.2 %fusion.6 = f32[512,1,128]{2,1,0:T(1,128)S(1)} fusion(bf16[512,128,128]{2,1,0:T(8,128)(2,1)} %param.6, bf16[512,128,1]{1,0,2:T(8,128)(2,1)S(1)} %bitcast.54), kind=kOutput, calls=%fused_computation.27 | convolution fusion | flops 16777216 | bytes 17170432 | tf_op jit(solution)/shard_map/tij,tj->ti/dot_general | solution.py:46
  201.1 8.1 %fusion.4 = f32[512,1,128]{2,1,0:T(1,128)S(1)} fusion(bf16[512,128,128]{2,1,0:T(8,128)(2,1)} %param.6, bf16[512,128,1]{1,0,2:T(8,128)(2,1)S(1)} %bitcast.61), kind=kOutput, calls=%fused_computation.25 | convolution fusion | flops 16777216 | bytes 17170432 | tf_op jit(solution)/shard_map/tij,ti->tj/dot_general | solution.py:53
  211.6 13.9 %all_to_all.36 = bf16[128,2,128]{2,1,0:T(2,128)(2,1)S(1)} all-to-all(bf16[128,2,128]{2,1,0:T(2,128)(2,1)S(1)} %bitcast.70), channel_id=1, replica_groups=mesh['src_0'=4,'src_1'=4,'reg_0'=4,'reg_1'=2] {'src_0','src_1','reg_0','..., dimensions={0} | all-to-all | bytes 131072 | tf_op jit(solution)/shard_map/all_to_all | solution.py:56
  227.7 7.5 %all-reduce.9 = (f32[]{:T(128)}, f32[]{:T(128)}, f32[]{:T(128)}, f32[]{:T(128)}) all-reduce(f32[]{:T(128)} %get-tuple-element.7, f32[]{:T(128)} %get-tuple-element.80, f32[]{:T(128)} %get-tuple-element.6, f32[]{:T(128)} %get-tuple-element.5), channel_id=1, replica_groups=mesh['src_0'=4,'src_1'=4,'reg_0'=4,'reg_1'=2] {'src_0'}, use_global_device_ids=true, to_apply=%region_53.0 | all-reduce | flops 4 | bytes 32 | tf_op jit(solution)/shard_map/psum | solution.py:17
  242.7 7.6 %all-reduce.1 = (f32[]{:T(128)}, f32[]{:T(128)}, f32[]{:T(128)}, f32[]{:T(128)}) all-reduce(f32[]{:T(128)} %get-tuple-element.33, f32[]{:T(128)} %get-tuple-element.34, f32[]{:T(128)} %get-tuple-element.35, f32[]{:T(128)} %get-tuple-element.36), channel_id=1, replica_groups=mesh['src_0'=4,'src_1'=4,'reg_0'=4,'reg_1'=2] {'reg_0'}, use_global_device_ids=true, to_apply=%region_55.0 | all-reduce | flops 4 | bytes 32 | tf_op jit(solution)/shard_map/psum | solution.py:17
  250.3 9.7 %all-reduce.13 = (f32[]{:T(128)}, f32[]{:T(128)}, f32[]{:T(128)}, f32[]{:T(128)}) all-reduce(f32[]{:T(128)} %get-tuple-element.17, f32[]{:T(128)} %get-tuple-element.18, f32[]{:T(128)} %get-tuple-element.19, f32[]{:T(128)} %get-tuple-element.20), channel_id=1, replica_groups=mesh['src_0'=4,'src_1'=4,'reg_0'=4,'reg_1'=2] {'reg_1'}, use_global_device_ids=true, to_apply=%region_56.0 | all-reduce | flops 4 | bytes 32 | tf_op jit(solution)/shard_map/psum | solution.py:17
  276.9 12.2 %fusion.2 = f32[512,1,128]{2,1,0:T(1,128)S(1)} fusion(bf16[512,128,128]{2,1,0:T(8,128)(2,1)} %param.6, bf16[512,128,1]{1,0,2:T(8,128)(2,1)S(1)} %bitcast.52), kind=kOutput, calls=%fused_computation.23 | convolution fusion | flops 16777216 | bytes 17170432 | tf_op jit(solution)/shard_map/tij,tj->ti/dot_general | solution.py:46
  294.6 8.1 %fusion = f32[512,1,128]{2,1,0:T(1,128)S(1)} fusion(bf16[512,128,128]{2,1,0:T(8,128)(2,1)} %param.6, bf16[512,128,1]{1,0,2:T(8,128)(2,1)S(1)} %bitcast.58), kind=kOutput, calls=%fused_computation.21 | convolution fusion | flops 16777216 | bytes 17170432 | tf_op jit(solution)/shard_map/tij,ti->tj/dot_general | solution.py:53
  311.0 8.8 %all-to-all-done.6 = bf16[128,2,128]{2,1,0:T(2,128)(2,1)S(1)} async-done(((bf16[128,2,128]{2,1,0:T(2,128)(2,1)}), bf16[128,2,128]{2,1,0:T(2,128)(2,1)S(1)}, u32[]{:S(2)}, u32[]{:S(2)}) %all-to-all-start.6) | async-done | bytes 65568 | tf_op jit(solution)/shard_map/all_to_all | solution.py:56
  322.0 7.5 %all-reduce.8 = (f32[]{:T(128)}, f32[]{:T(128)}, f32[]{:T(128)}, f32[]{:T(128)}) all-reduce(f32[]{:T(128)} %multiply_reduce_fusion.11, f32[]{:T(128)} %get-tuple-element.4, f32[]{:T(128)} %get-tuple-element.3, f32[]{:T(128)} %get-tuple-element.2), channel_id=1, replica_groups=mesh['src_0'=4,'src_1'=4,'reg_0'=4,'reg_1'=2] {'src_0'}, use_global_device_ids=true, to_apply=%region_69.0 | all-reduce | flops 4 | bytes 32 | tf_op jit(solution)/shard_map/psum | solution.py:17
  336.9 7.6 %all-reduce = (f32[]{:T(128)}, f32[]{:T(128)}, f32[]{:T(128)}, f32[]{:T(128)}) all-reduce(f32[]{:T(128)} %get-tuple-element.29, f32[]{:T(128)} %get-tuple-element.30, f32[]{:T(128)} %get-tuple-element.31, f32[]{:T(128)} %get-tuple-element.32), channel_id=1, replica_groups=mesh['src_0'=4,'src_1'=4,'reg_0'=4,'reg_1'=2] {'reg_0'}, use_global_device_ids=true, to_apply=%region_71.0 | all-reduce | flops 4 | bytes 32 | tf_op jit(solution)/shard_map/psum | solution.py:17
  344.5 9.5 %all-reduce.12 = (f32[]{:T(128)}, f32[]{:T(128)}, f32[]{:T(128)}, f32[]{:T(128)}) all-reduce(f32[]{:T(128)} %get-tuple-element.13, f32[]{:T(128)} %get-tuple-element.14, f32[]{:T(128)} %get-tuple-element.15, f32[]{:T(128)} %get-tuple-element.16), channel_id=1, replica_groups=mesh['src_0'=4,'src_1'=4,'reg_0'=4,'reg_1'=2] {'reg_1'}, use_global_device_ids=true, to_apply=%region_72.0 | all-reduce | flops 4 | bytes 32 | tf_op jit(solution)/shard_map/psum | solution.py:17
  (67 shorter events, 115.6 us)
Async XLA Ops:
  0.6 12.2 %copy-start.1 = (s32[512]{0:T(512)S(1)}, s32[512]{0:T(512)}, u32[]{:S(2)}) copy-start(s32[512]{0:T(512)} %param.9) | copy-start | bytes 6148
  0.6 26.8 %copy-start.2 = (s32[1,128,2]{1,2,0:T(2,128)S(1)}, s32[1,128,2]{1,2,0:T(2,128)}, u32[]{:S(2)}) copy-start(s32[1,128,2]{1,2,0:T(2,128)} %param.11) | copy-start | bytes 3076
  15.9 20.9 %all-to-all-start = ((bf16[128,2,128]{2,1,0:T(2,128)(2,1)}), bf16[128,2,128]{2,1,0:T(2,128)(2,1)S(1)}, u32[]{:S(2)}, u32[]{:S(2)}) async-start(bf16[128,2,128]{2,1,0:T(2,128)(2,1)} %bitcast.4), calls=%async_computation | async-start | bytes 131072 | tf_op jit(solution)/shard_map/all_to_all | solution.py:56
  73.8 13.6 %all-to-all-start.1 = ((bf16[128,2,128]{2,1,0:T(2,128)(2,1)}), bf16[128,2,128]{2,1,0:T(2,128)(2,1)S(1)}, u32[]{:S(2)}, u32[]{:S(2)}) async-start(bf16[128,2,128]{2,1,0:T(2,128)(2,1)} %bitcast.7), calls=%async_computation.1 | async-start | bytes 131072 | tf_op jit(solution)/shard_map/all_to_all | solution.py:42
  88.7 16.3 %copy-start = (f32[64,128]{1,0:T(8,128)S(1)}, f32[64,128]{1,0:T(8,128)}, u32[]{:S(2)}) copy-start(f32[64,128]{1,0:T(8,128)} %param.7) | copy-start | bytes 98308
  167.9 13.5 %all-to-all-start.3 = ((bf16[128,2,128]{2,1,0:T(2,128)(2,1)}), bf16[128,2,128]{2,1,0:T(2,128)(2,1)S(1)}, u32[]{:S(2)}, u32[]{:S(2)}) async-start(bf16[128,2,128]{2,1,0:T(2,128)(2,1)} %bitcast.17), calls=%async_computation.3 | async-start | bytes 131072 | tf_op jit(solution)/shard_map/all_to_all | solution.py:42
  262.2 13.3 %all-to-all-start.5 = ((bf16[128,2,128]{2,1,0:T(2,128)(2,1)}), bf16[128,2,128]{2,1,0:T(2,128)(2,1)S(1)}, u32[]{:S(2)}, u32[]{:S(2)}) async-start(bf16[128,2,128]{2,1,0:T(2,128)(2,1)} %bitcast.27), calls=%async_computation.5 | async-start | bytes 131072 | tf_op jit(solution)/shard_map/all_to_all | solution.py:42
  305.7 14.1 %all-to-all-start.6 = ((bf16[128,2,128]{2,1,0:T(2,128)(2,1)}), bf16[128,2,128]{2,1,0:T(2,128)(2,1)S(1)}, u32[]{:S(2)}, u32[]{:S(2)}) async-start(bf16[128,2,128]{2,1,0:T(2,128)(2,1)} %bitcast.35), calls=%async_computation.6 | async-start | bytes 131072 | tf_op jit(solution)/shard_map/all_to_all | solution.py:56
where the time goes:
time: 366 us; the launch traced here: 359 us
  blocking collectives  157 us (43%)
  matrix products  68.9 us (19%)
  other arithmetic  37 us (10%)
  waiting for transfers between devices  36.1 us (10%)
  starting transfers between devices  27.8 us (8%)
  between operations  18.7 us (5%)
  local copies, waits for them, and re-layouts  14.2 us (4%)
    psum x16, blocking collectives, over_axes(): value = lax.psum(value, axis)  129 us
    dot_general x3, matrix products, per_device(): jnp.einsum('tij,tj->ti', tiles, forward_picked, preferred_element_type=jn...  36.6 us
    dot_general x4, matrix products, per_device(): jnp.einsum('tij,ti->tj', tiles, picked, preferred_element_type=jnp.float32)  32.3 us
    all_to_all x2, blocking collectives, per_device(): lax.all_to_all(slot_sums.astype(jnp.bfloat16), SRC_REG, split_axis=0, con...  27.9 us
    all_to_all x3, waiting for transfers between devices, per_device(): lax.all_to_all(outgoing, SRC_REG, split_axis=0, concat_axis=0, tiled=True)  18.3 us
    all_to_all x2, waiting for transfers between devices, per_device(): lax.all_to_all(slot_sums.astype(jnp.bfloat16), SRC_REG, split_axis=0, con...  17.8 us
    all_to_all x2, starting transfers between devices, per_device(): lax.all_to_all(slot_sums.astype(jnp.bfloat16), SRC_REG, split_axis=0, con...  16.1 us
    scatter-add x3, other arithmetic, per_device(): jax.ops.segment_sum(product, tile_rows, num_segments=row_blocks) / alpha  12.3 us
  transfers between devices with their start and end apart: 5, of which 5 were waited for; matrix products, arithmetic and copies ran while one was open for 0% of the time, Pallas kernels for 0%

commit v1 on v0

v1 whole, which is shorter than its diff:
```python
import functools

import jax
import jax.numpy as jnp
from jax import lax
from jax.experimental import pallas as pl
from jax.experimental.pallas import tpu as pltpu
from jax.sharding import Mesh
from jax.sharding import PartitionSpec as P

BLK_DEV = 256
ITERS = 3
AXES = ("src_0", "src_1", "reg_0", "reg_1")
damping = 0.5

F32 = jnp.float32
BF16 = jnp.bfloat16
ROWS = 4
UNROLL = 64


def iota(shape, axis):
    return lax.broadcasted_iota(jnp.int32, shape, axis)


def dot(a, b, dims=((1,), (0,))):
    return lax.dot_general(a, b, (dims, ((), ())), preferred_element_type=F32)


def two_pieces(x):
    hi = x.astype(BF16)
    lo = (x - hi.astype(F32)).astype(BF16)
    return jnp.concatenate([hi, lo], axis=1)


def exact_dot(onehot, x):
    width = x.shape[1]
    both = dot(onehot, two_pieces(x))
    return both[:, :width] + both[:, width:]


def scalar_row(x, rows, width):
    a = x.astype(BF16).astype(F32)
    b = (x - a).astype(BF16).astype(F32)
    c = x - a - b
    lane = iota((rows, width), 1)
    row = iota((rows, width), 0) & (ROWS - 1)
    v = jnp.where(lane == 0, a, jnp.where(lane == 1, b, jnp.where(lane == 2, c, 0.0)))
    return jnp.where(row == 2, v, 0.0)


def scalar_total(recv):
    rows, width = recv.shape
    lane = iota((rows, width), 1)
    row = iota((rows, width), 0) & (ROWS - 1)
    return total(jnp.where((row == 2) & (lane < 3), recv.astype(F32), 0.0))


def total(x):
    return jnp.sum(jnp.sum(x, axis=0, keepdims=True), axis=1, keepdims=True)


def products(picked_ref, tiles_ref, out_ref, first, transposed):
    row = iota((16, 128), 0)
    if transposed:
        left = ((row & 3) < 2).astype(BF16)
    else:
        left = ((row & 1) == 0).astype(BF16)
    right = 1 - left
    row8 = iota((8, 128), 0)
    low = row8 < 4
    if transposed:
        side = (row8 & 1) == 0
    else:
        side = (row8 & 3) < 2
    dims = ((1,), (1,)) if transposed else ((1,), (0,))
    for pack in range(UNROLL // 16):
        base = first + 16 * pack
        pk = picked_ref[pl.ds(base, 16), :]
        lhs = jnp.concatenate([pk * left, pk * right], axis=1)
        res = []
        for g in range(4):
            wa = tiles_ref[pl.ds(base + 4 * g, 2)].reshape(256, 128)
            wb = tiles_ref[pl.ds(base + 4 * g + 2, 2)].reshape(256, 128)
            res.append(dot(lhs, jnp.concatenate([wa, wb], axis=1), dims))
        for h in range(2):
            a = res[2 * h][8 * h : 8 * h + 8]
            b = res[2 * h + 1][8 * h : 8 * h + 8]
            a = jnp.where(side, a[:, :128], a[:, 128:])
            b = jnp.where(side, b[:, :128], b[:, 128:])
            out_ref[pl.ds(base + 8 * h, 8), :] = jnp.where(low, a, b)


def first_kernel(
    count_ref, tiles_ref, rays_ref, rows_ref, slots_ref, req_ref,
    tiles_out, send_ref, s_ref, st_ref, r_ref, rt_ref, g_ref, gt_ref,
    picked, res, sem,
):
    ntile = tiles_ref.shape[0]
    nrow = rays_ref.shape[0]
    steps = ntile // UNROLL

    def copy(i):
        part = pl.ds(i * UNROLL, UNROLL)
        return pltpu.make_async_copy(tiles_ref.at[part], tiles_out.at[part], sem.at[i])

    for i in range(steps):
        copy(i).start()
    live = iota((1, ntile), 1) < count_ref[0]
    rows = jnp.where(live, rows_ref[...], -1)
    slots = slots_ref[...]
    slots = jnp.where(live, (slots >> 1) * ROWS + (slots & 1), -1)
    rt = (jnp.broadcast_to(rows, (nrow, ntile)) == iota((nrow, ntile), 0)).astype(F32)
    rt_ref[...] = rt.astype(BF16)
    rb = jnp.broadcast_to(rows.astype(F32), (128, ntile)).T.astype(jnp.int32)
    r_ref[...] = (rb == iota((ntile, 128), 1)).astype(F32).astype(BF16)
    nq = st_ref.shape[0]
    for q in range(0, nq, 128):
        st = jnp.broadcast_to(slots, (128, ntile)) == iota((128, ntile), 0) + q
        st_ref[q : q + 128, :] = st.astype(F32).astype(BF16)
    sb = jnp.broadcast_to(slots.astype(F32), (128, ntile)).T.astype(jnp.int32)
    for q in range(0, nq, 128):
        s = sb == iota((ntile, 128), 1) + q
        s_ref[:, q : q + 128] = s.astype(F32).astype(BF16)
    req = req_ref[...]
    gt = jnp.broadcast_to(req, (BLK_DEV, nq)) == iota((BLK_DEV, nq), 0)
    gt_ref[...] = gt.astype(F32).astype(BF16)
    gb = jnp.broadcast_to(req.astype(F32), (128, nq)).T.astype(jnp.int32)
    for q in range(0, BLK_DEV, 128):
        g = gb == iota((nq, 128), 1) + q
        g_ref[:, q : q + 128] = g.astype(F32).astype(BF16)

    uraw = rays_ref[...]
    ub = jnp.concatenate([uraw, jnp.zeros((128 - nrow, 128), F32)], axis=0).astype(BF16)
    picked[...] = dot(r_ref[...], ub).astype(BF16)
    uu = total(uraw * uraw)

    def body(i, carry):
        copy(i).wait()
        products(picked, tiles_out, res, i * UNROLL, False)
        return carry

    lax.fori_loop(0, steps, body, 0)
    sums = exact_dot(st_ref[...], res[...])
    send_ref[...] = (sums + scalar_row(uu, nq, 128)).astype(BF16)


def ray_kernel(
    tiles_ref, recv_ref, s_ref, st_ref, r_ref, rt_ref, uraw_ref, beta_ref,
    send_ref, uraw_out, alpha_ref,
    picked, res,
):
    ntile = tiles_ref.shape[0]
    nrow = uraw_ref.shape[0]
    nq = recv_ref.shape[0]
    steps = ntile // UNROLL
    recv = recv_ref[...]
    alpha = jnp.sqrt(scalar_total(recv))
    picked[...] = dot(s_ref[...], recv).astype(BF16)

    def forward(i, carry):
        products(picked, tiles_ref, res, i * UNROLL, True)
        return carry

    lax.fori_loop(0, steps, forward, 0)
    product = exact_dot(rt_ref[...], res[...])
    beta = beta_ref[0:1, 0:1]
    uraw = product / alpha - alpha * (uraw_ref[...] / beta)
    uraw_out[...] = uraw
    alpha_ref[...] = jnp.broadcast_to(alpha, (8, 128))
    ub = jnp.concatenate([uraw, jnp.zeros((128 - nrow, 128), F32)], axis=0).astype(BF16)
    picked[...] = dot(r_ref[...], ub).astype(BF16)
    uu = total(uraw * uraw)

    def adjoint(i, carry):
        products(picked, tiles_ref, res, i * UNROLL, False)
        return carry

    lax.fori_loop(0, steps, adjoint, 0)
    sums = exact_dot(st_ref[...], res[...])
    send_ref[...] = (sums + scalar_row(uu, nq, 128)).astype(BF16)


def cell_kernel(step, last, *refs):
    recv_ref, gt_ref, g_ref = refs[:3]
    recv = recv_ref[...]
    nq = recv.shape[0]
    beta = jnp.sqrt(scalar_total(recv))
    grad = dot(gt_ref[...], recv)
    if step == 0:
        send_ref, vraw_out, state_out = refs[3:]
        vraw = grad / beta
        zero = jnp.zeros_like(beta)
        state = [beta, beta, zero, zero, zero, zero]
    else:
        if step == 1:
            vraw_ref, alpha_ref, state_ref = refs[3:6]
            w_ref = solution_ref = None
            outs = refs[6:]
        elif step == 2:
            vraw_ref, alpha_ref, state_ref, w_ref, solution_ref = refs[3:8]
            outs = refs[8:]
        else:
            vraw_ref, alpha_ref, state_ref, w_ref, solution_ref = refs[3:8]
            outs = refs[8:]
        alpha = alpha_ref[0:1, 0:1]
        old = [state_ref[i : i + 1, 0:1] for i in range(6)]
        _, phibar, rhobar, cosine, sine, rho = old
        v = vraw_ref[...] / alpha
        vraw = grad / beta - beta * v
        if step == 1:
            w = v
            rhobar = alpha
        else:
            w = v - (sine * alpha / rho) * w_ref[...]
            rhobar = -cosine * alpha
        rhobar1 = jnp.sqrt(rhobar * rhobar + damping * damping)
        phibar = rhobar / rhobar1 * phibar
        rho = jnp.sqrt(rhobar1 * rhobar1 + beta * beta)
        cosine = rhobar1 / rho
        sine = beta / rho
        phi = cosine * phibar
        phibar = sine * phibar
        update = (phi / rho) * w
        solution = update if step == 1 else solution_ref[...] + update
        if last:
            send_ref, vraw_out, solution_out = outs
            solution_out[...] = solution
        else:
            send_ref, vraw_out, state_out, w_out, solution_out = outs
            solution_out[...] = solution
            w_out[...] = w
            state = [beta, phibar, rhobar, cosine, sine, rho]
    vraw_out[...] = vraw
    vv = total(vraw * vraw)
    if last:
        send_ref[...] = jnp.broadcast_to(vv, send_ref.shape)
    else:
        sent = dot(g_ref[...], vraw.astype(BF16))
        send_ref[...] = (sent + scalar_row(vv, nq, 128)).astype(BF16)
        for i, x in enumerate(state):
            state_out[i : i + 1, :] = jnp.broadcast_to(x, (1, 128))


def norm_kernel(scale, recv_ref, vraw_ref, out_ref):
    recv = recv_ref[...]
    vv = jnp.sum(jnp.sum(recv, axis=0, keepdims=True)[:, 0:1], axis=1, keepdims=True)
    out_ref[...] = vraw_ref[...] * (scale / jnp.sqrt(vv))


def shape(dims, dtype=F32):
    return jax.ShapeDtypeStruct(dims, dtype)


def vmem(dims, dtype):
    return pltpu.VMEM(dims, dtype)


def call(kernel, outs, n_in, scratch=(), limit=24 << 20, flops=0, smem=0, hbm=None):
    in_specs = []
    for i in range(n_in):
        if i < smem:
            in_specs.append(pl.BlockSpec(memory_space=pltpu.SMEM))
        elif i == hbm:
            in_specs.append(pl.BlockSpec(memory_space=pl.ANY))
        else:
            in_specs.append(pl.BlockSpec(memory_space=pltpu.VMEM))
    return pl.pallas_call(
        kernel,
        out_shape=outs,
        in_specs=in_specs,
        out_specs=[pl.BlockSpec(memory_space=pltpu.VMEM)] * len(outs),
        scratch_shapes=list(scratch),
        compiler_params=pltpu.CompilerParams(vmem_limit_bytes=limit),
    )


def per_device(tiles, rays, tile_rows, tile_slots, tile_count, wanted):
    ndev = lax.axis_size(AXES)
    ntile, _, width = tiles.shape
    nrow = rays.shape[0]
    cap = wanted.shape[2]
    nq = ndev * ROWS
    req = jnp.concatenate(
        [wanted[0], jnp.full((ndev, ROWS - cap), -1, jnp.int32)], axis=1
    ).reshape(1, nq)

    def exchange(x):
        rows = x.shape[0] // ndev
        y = lax.all_to_all(
            x.reshape(ndev, rows, width), AXES, split_axis=0, concat_axis=0, tiled=True
        )
        return y.reshape(x.shape)

    scratch = [pltpu.VMEM((ntile, width), BF16), pltpu.VMEM((ntile, width), F32)]
    tiles_v, send, s, st, r, rt, g, gt = call(
        first_kernel,
        [
            vmem((ntile, width, width), BF16),
            shape((nq, width), BF16),
            shape((ntile, nq), BF16),
            shape((nq, ntile), BF16),
            shape((ntile, 128), BF16),
            shape((nrow, ntile), BF16),
            shape((nq, BLK_DEV), BF16),
            shape((BLK_DEV, nq), BF16),
        ],
        6,
        scratch + [pltpu.SemaphoreType.DMA((ntile // UNROLL,))],
        smem=1,
        hbm=1,
    )(tile_count, tiles, rays, tile_rows.reshape(1, ntile), tile_slots.reshape(1, ntile), req)

    cells = shape((BLK_DEV, width))
    state_shape = shape((8, width))
    sent = shape((nq, width), BF16)
    uraw = rays
    w = solution = alpha = state = vraw = None
    for step in range(ITERS + 1):
        last = step == ITERS
        if step > 0:
            recv = exchange(send)
            send, uraw, alpha = call(
                ray_kernel,
                [sent, shape((nrow, width)), state_shape],
                8,
                scratch,
            )(pltpu.with_memory_space_constraint(tiles_v, pltpu.VMEM), recv, s, st, r, rt, uraw, state)
        recv = exchange(send)
        if step == 0:
            send, vraw, state = call(
                functools.partial(cell_kernel, step, False), [sent, cells, state_shape], 3
            )(recv, gt, g)
        elif last:
            send, vraw, solution = call(
                functools.partial(cell_kernel, step, True),
                [shape((ndev, width)), cells, cells],
                8,
            )(recv, gt, g, vraw, alpha, state, w, solution)
        else:
            extra = [] if step == 1 else [w, solution]
            send, vraw, state, w, solution = call(
                functools.partial(cell_kernel, step, False),
                [sent, cells, state_shape, cells, cells],
                6 + len(extra),
            )(recv, gt, g, vraw, alpha, state, *extra)
    recv = exchange(send)
    scale = float(BLK_DEV * width * ndev) ** 0.5
    (right,) = call(functools.partial(norm_kernel, scale), [cells], 2)(recv, vraw)
    return (solution, right)


def solution(mesh):
    split = Mesh(mesh.devices.reshape(4, 4, 4, 2), AXES)
    placed = (
        P(AXES, None, None),
        P(AXES, None),
        P(AXES),
        P(AXES),
        P(AXES),
        P(AXES, None, None),
    )
    return jax.shard_map(
        per_device,
        mesh=split,
        in_specs=placed,
        out_specs=(P(AXES, None), P(AXES, None)),
        check_vma=False,
    )
```

time: 366 us -> 164 us (0.45); the launches traced: 359 us -> 163 us
  matrix products: 68.9 us -> 0 us
  Pallas kernels: 0 us -> 38.5 us
  other arithmetic: 37 us -> 0 us
  waiting for transfers between devices: 36.1 us -> 0 us
  blocking collectives: 157 us -> 121 us
  starting transfers between devices: 27.8 us -> 0 us
  between operations: 18.7 us -> 1.33 us
  local copies, waits for them, and re-layouts: 14.2 us -> 3.02 us
    psum x16 -> x0, blocking collectives: 129 us -> none  [over_axes(): value = lax.psum(value, axis)]
    all_to_all x2 -> x8, blocking collectives: 27.9 us -> 121 us  [exchange(): lax.all_to_all(x.reshape(ndev, rows, width), AXES, split_axis=0, concat_a...]
    dot_general x7 -> x0, matrix products: 68.9 us -> none  [the longest x3 36.6 us: per_device(): jnp.einsum('tij,tj->ti', tiles, forward_picked, preferred_element_type=jn...]
    pallas_call x0 -> x9, Pallas kernels: none -> 38.5 us  [the longest x3 28.4 us: per_device(): call(ray_kernel, [sent, shape((nrow, width)), state_shape], 8, scratch)]
    all_to_all x5 -> x0, waiting for transfers between devices: 36.1 us -> none  [the longest x3 18.3 us: per_device(): lax.all_to_all(outgoing, SRC_REG, split_axis=0, concat_axis=0, tiled=True)]
    scatter-add x11 -> x0, other arithmetic: 27.8 us -> none  [the longest x3 12.3 us: per_device(): jax.ops.segment_sum(product, tile_rows, num_segments=row_blocks) / alpha]
    all_to_all x5 -> x0, starting transfers between devices: 27.8 us -> none  [the longest x2 16.1 us: per_device(): lax.all_to_all(slot_sums.astype(jnp.bfloat16), SRC_REG, split_axis=0, con...]
    gather x10 -> x0, local copies, waits for them, and re-layouts: 13.8 us -> none  [the longest x4 5.35 us: per_device(): picked = uraw.astype(jnp.bfloat16)[tile_rows]]
  transfers between devices with their start and end apart: 5 -> 0, of which waited for: 5 -> 0; matrix products, arithmetic and copies ran while one was open for 0% -> 0% of each run, Pallas kernels for 0% -> 0%
where the time goes in v1:
time: 164 us; the launch traced here: 163 us
  blocking collectives  121 us (74%)
  Pallas kernels  38.5 us (23%)
  local copies, waits for them, and re-layouts  3.02 us (2%)
    all_to_all x8, blocking collectives, exchange(): lax.all_to_all(x.reshape(ndev, rows, width), AXES, split_axis=0, concat_a...  121 us
    pallas_call x3, Pallas kernels, per_device(): call(ray_kernel, [sent, shape((nrow, width)), state_shape], 8, scratch)  28.4 us
    pallas_call x1, Pallas kernels, per_device(): call(first_kernel, [vmem((ntile, width, width), BF16), shape((nq, width),...  7.07 us

profile of v1, /device:TPU:1, one launch (start us, length us, event | category | flops | bytes accessed | tf_op | source)
XLA Modules:
  0.0 163.5 jit_solution(2284231387110192036)
XLA Ops:
  1.3 0.8 copy.12
  2.1 0.1 reshape.63.req_ref
  2.2 0.0 copy-start
  2.2 0.8 copy-done
  2.9 0.0 copy-start.1
  2.9 0.7 copy-done.1
  3.6 0.7 copy-done.2
  4.3 7.1 %shard_map.77 = (bf16[512,128,128]{2,1,0:T(8,128)(2,1)S(1)}, bf16[512,128]{1,0:T(8,128)(2,1)S(1)}, bf16[512,512]{1,0:T(8,128)(2,1)S(1)}, bf16[512,512]{1,0:T(8,1...) custom-call(s32[1]{0:T(128)S(6)} %copy.13.count_ref, ...), custom_call_target="tpu_custom_call" | custom-call | tf_op jit(solution)/shard_map/pallas_call | solution.py:296
  11.4 21.3 %all_to_all.40 = bf16[128,4,128]{2,1,0:T(4,128)(2,1)S(1)} all-to-all(bf16[128,4,128]{2,1,0:T(4,128)(2,1)S(1)} %bitcast.30), channel_id=1, replica_groups=mesh['src_0'=4,'src_1'=4,'reg_0'=4,'reg_1'=2] {'src_0','src_1','reg_0','..., dimensions={0} | all-to-all | bytes 262144 | tf_op jit(solution)/shard_map/all_to_all | solution.py:290
  32.7 0.4 shard_map.78
  33.2 14.3 %all_to_all.41 = bf16[128,4,128]{2,1,0:T(4,128)(2,1)S(1)} all-to-all(bf16[128,4,128]{2,1,0:T(4,128)(2,1)S(1)} %bitcast.34), channel_id=1, replica_groups=mesh['src_0'=4,'src_1'=4,'reg_0'=4,'reg_1'=2] {'src_0','src_1','reg_0','..., dimensions={0} | all-to-all | bytes 262144 | tf_op jit(solution)/shard_map/all_to_all | solution.py:290
  47.4 9.4 %shard_map.79 = (bf16[512,128]{1,0:T(8,128)(2,1)S(1)}, f32[64,128]{1,0:T(8,128)S(1)}, f32[8,128]{1,0:T(8,128)S(1)}) custom-call(bf16[512,128,128]{2,1,0:T(8,128)(2,1)S(1)} %get-tuple-element.34.tiles_ref, bf16[512,128]{1,0:T(8,128)(2,1)S(1)} %bitcast.23, bf16[512,512]{1,0:T(8,128)(2,1)S(1)} %get-tuple-element.39.s_ref, ...), custom_call_target="tpu_custom_call" | custom-call | tf_op jit(solution)/shard_map/pallas_call | solution.py:323
  56.8 14.3 %all_to_all.42 = bf16[128,4,128]{2,1,0:T(4,128)(2,1)S(1)} all-to-all(bf16[128,4,128]{2,1,0:T(4,128)(2,1)S(1)} %bitcast.35), channel_id=1, replica_groups=mesh['src_0'=4,'src_1'=4,'reg_0'=4,'reg_1'=2] {'src_0','src_1','reg_0','..., dimensions={0} | all-to-all | bytes 262144 | tf_op jit(solution)/shard_map/all_to_all | solution.py:290
  71.1 0.4 shard_map.80
  71.6 14.3 %all_to_all.43 = bf16[128,4,128]{2,1,0:T(4,128)(2,1)S(1)} all-to-all(bf16[128,4,128]{2,1,0:T(4,128)(2,1)S(1)} %bitcast.32), channel_id=1, replica_groups=mesh['src_0'=4,'src_1'=4,'reg_0'=4,'reg_1'=2] {'src_0','src_1','reg_0','..., dimensions={0} | all-to-all | bytes 262144 | tf_op jit(solution)/shard_map/all_to_all | solution.py:290
  85.8 9.4 %shard_map.81 = (bf16[512,128]{1,0:T(8,128)(2,1)S(1)}, f32[64,128]{1,0:T(8,128)S(1)}, f32[8,128]{1,0:T(8,128)S(1)}) custom-call(bf16[512,128,128]{2,1,0:T(8,128)(2,1)S(1)} %get-tuple-element.34.tiles_ref, bf16[512,128]{1,0:T(8,128)(2,1)S(1)} %bitcast.22, bf16[512,512]{1,0:T(8,128)(2,1)S(1)} %get-tuple-element.39.s_ref, ...), custom_call_target="tpu_custom_call" | custom-call | tf_op jit(solution)/shard_map/pallas_call | solution.py:323
  95.2 14.3 %all_to_all.44 = bf16[128,4,128]{2,1,0:T(4,128)(2,1)S(1)} all-to-all(bf16[128,4,128]{2,1,0:T(4,128)(2,1)S(1)} %bitcast.33), channel_id=1, replica_groups=mesh['src_0'=4,'src_1'=4,'reg_0'=4,'reg_1'=2] {'src_0','src_1','reg_0','..., dimensions={0} | all-to-all | bytes 262144 | tf_op jit(solution)/shard_map/all_to_all | solution.py:290
  109.5 0.4 shard_map.82
  109.9 14.3 %all_to_all.45 = bf16[128,4,128]{2,1,0:T(4,128)(2,1)S(1)} all-to-all(bf16[128,4,128]{2,1,0:T(4,128)(2,1)S(1)} %bitcast.29), channel_id=1, replica_groups=mesh['src_0'=4,'src_1'=4,'reg_0'=4,'reg_1'=2] {'src_0','src_1','reg_0','..., dimensions={0} | all-to-all | bytes 262144 | tf_op jit(solution)/shard_map/all_to_all | solution.py:290
  124.2 9.6 %shard_map.83 = (bf16[512,128]{1,0:T(8,128)(2,1)S(1)}, f32[64,128]{1,0:T(8,128)}, f32[8,128]{1,0:T(8,128)S(1)}) custom-call(bf16[512,128,128]{2,1,0:T(8,128)(2,1)S(1)} %get-tuple-element.34.tiles_ref, bf16[512,128]{1,0:T(8,128)(2,1)S(1)} %bitcast.21, bf16[512,512]{1,0:T(8,128)(2,1)S(1)} %get-tuple-element.39.s_ref, ...), custom_call_target="tpu_custom_call" | custom-call | tf_op jit(solution)/shard_map/pallas_call | solution.py:323
  133.8 14.3 %all_to_all.46 = bf16[128,4,128]{2,1,0:T(4,128)(2,1)S(1)} all-to-all(bf16[128,4,128]{2,1,0:T(4,128)(2,1)S(1)} %bitcast.31), channel_id=1, replica_groups=mesh['src_0'=4,'src_1'=4,'reg_0'=4,'reg_1'=2] {'src_0','src_1','reg_0','..., dimensions={0} | all-to-all | bytes 262144 | tf_op jit(solution)/shard_map/all_to_all | solution.py:290
  148.0 0.9 shard_map.84
  149.0 13.7 %all_to_all.47 = f32[128,1,128]{2,1,0:T(1,128)S(1)} all-to-all(f32[128,1,128]{2,1,0:T(1,128)S(1)} %bitcast.36), channel_id=1, replica_groups=mesh['src_0'=4,'src_1'=4,'reg_0'=4,'reg_1'=2] {'src_0','src_1','reg_0','..., dimensions={0} | all-to-all | bytes 131072 | tf_op jit(solution)/shard_map/all_to_all | solution.py:290
  162.7 0.8 shard_map.85
  (2 shorter events, 0.0 us)
Async XLA Ops:
  2.2 0.8 copy-start
  2.9 0.7 copy-start.1
  3.6 0.7 copy-start.2

commit v2 on v0

v2 whole, which is shorter than its diff:
```python
import functools

import jax
import jax.numpy as jnp
from jax import lax
from jax.experimental import pallas as pl
from jax.experimental.pallas import tpu as pltpu
from jax.sharding import Mesh
from jax.sharding import PartitionSpec as P

BLK_DEV = 256
ITERS = 3
AXES = ("src_0", "src_1", "reg_0", "reg_1")
damping = 0.5

F32 = jnp.float32
BF16 = jnp.bfloat16
ROWS = 4
UNROLL = 128
CHUNK = 32
DEPTH = 4
FIRST_UNROLL = 64
PARTS = 2
EXTRA = 16


def iota(shape, axis):
    return lax.broadcasted_iota(jnp.int32, shape, axis)


def onehot(x):
    return x.astype(F32).astype(BF16)


def dot(a, b, dims=((1,), (0,))):
    return lax.dot_general(a, b, (dims, ((), ())), preferred_element_type=F32)


def exact_dot(matrix, x):
    hi = x.astype(BF16)
    lo = (x - hi.astype(F32)).astype(BF16)
    both = dot(matrix, jnp.concatenate([hi, lo], axis=1))
    width = x.shape[1]
    return both[:, :width] + both[:, width:]


def with_scalar(sums, x):
    a = x.astype(BF16).astype(F32)
    b = (x - a).astype(BF16).astype(F32)
    c = x - a - b
    lane = iota((1, 8, 128), 2)
    row = iota((1, 8, 128), 1) & (ROWS - 1)
    v = jnp.where(lane == 0, a, jnp.where(lane == 1, b, jnp.where(lane == 2, c, 0.0)))
    out = jnp.where(row == 2, v, sums.reshape(-1, 8, 128))
    return out.reshape(sums.shape).astype(BF16)


def scalar_total(row):
    return jnp.sum(jnp.where(iota((1, 128), 1) < 3, row, 0.0), axis=1, keepdims=True)


def received_total(recv):
    rows = jnp.sum(recv.astype(F32).reshape(-1, 8, 128), axis=0)
    scalar = (iota((8, 128), 0) & (ROWS - 1) == 2) & (iota((8, 128), 1) < 3)
    return total(jnp.where(scalar, rows, 0.0))


def total(x):
    return jnp.sum(jnp.sum(x, axis=0, keepdims=True), axis=1, keepdims=True)


def products(picked_ref, tiles_ref, out_ref, first, offset, number):
    row = iota((16, 128), 0)
    left = onehot((row & 1) == 0)
    right = 1 - left
    row8 = iota((8, 128), 0)
    low = row8 < 4
    side = (row8 & 3) < 2
    for pack in range(number // 16):
        base = first + 16 * pack
        pk = picked_ref[pl.ds(base + offset, 16), :]
        lhs = jnp.concatenate([pk * left, pk * right], axis=1)
        res = []
        for g in range(4):
            at = base + 4 * g
            wa = tiles_ref[pl.ds(at, 2)].reshape(256, 128)
            wb = tiles_ref[pl.ds(at + 2, 2)].reshape(256, 128)
            res.append(dot(lhs, jnp.concatenate([wa, wb], axis=1)))
        for h in range(2):
            a = res[2 * h][8 * h : 8 * h + 8]
            b = res[2 * h + 1][8 * h : 8 * h + 8]
            a = jnp.where(side, a[:, :128], a[:, 128:])
            b = jnp.where(side, b[:, :128], b[:, 128:])
            out_ref[pl.ds(base + offset + 8 * h, 8), :] = jnp.where(low, a, b)


def first_kernel(
    count_ref, tiles_ref, rays_ref, rows_ref, slots_ref, wanted_ref,
    *refs,
):
    tiles, turned, refs = refs[:PARTS], refs[PARTS : 2 * PARTS], refs[2 * PARTS :]
    send_ref, rays, st_ref, rt_ref, s_ref, r_ref, g_ref, gt_ref = refs[:8]
    rows, slots, wanted, picked, res, sem, small_sem = refs[8:]
    ntile = tiles_ref.shape[0]
    nrow = rays_ref.shape[0]
    nq = st_ref.shape[0]
    cap, ndev = wanted_ref.shape

    part = ntile // PARTS
    copies = part // CHUNK

    def copy(p, i):
        src = tiles_ref.at[pl.ds(p * part + i * CHUNK, CHUNK)]
        return pltpu.make_async_copy(src, tiles[p].at[pl.ds(i * CHUNK, CHUNK)], sem.at[p, i])

    pairs = ((rows_ref, rows), (rays_ref, rays), (slots_ref, slots), (wanted_ref, wanted))
    small = [pltpu.make_async_copy(a, b, small_sem.at[i]) for i, (a, b) in enumerate(pairs)]
    for c in small:
        c.start()
    for i in range(DEPTH):
        copy(0, i).start()
    for c in small:
        c.wait()
    live = iota((1, ntile), 1) < count_ref[0]
    row_of = jnp.where(live, rows[...], -1)
    slot_of = slots[...]
    slot_of = jnp.where(live, (slot_of >> 1) * ROWS + (slot_of & 1), -1)
    rt = onehot(jnp.broadcast_to(row_of, (nrow, ntile)) == iota((nrow, ntile), 0))
    rt_ref[...] = rt
    r_ref[...] = rt.T
    uraw = rays[...]
    picked[...] = dot(r_ref[...], uraw.astype(BF16)).astype(BF16)
    uu = total(uraw * uraw)
    for q in range(0, nq, 128):
        st = jnp.broadcast_to(slot_of, (128, ntile)) == iota((128, ntile), 0) + q
        st = onehot(st)
        st_ref[q : q + 128, :] = st
        s_ref[:ntile, q : q + 128] = st.T
    scalar = (iota((EXTRA, nq), 1) & (ROWS - 1) == 2) & (iota((EXTRA, nq), 0) == 0)
    scalar = onehot(scalar)
    s_ref[ntile:, :] = scalar
    req = wanted[...].astype(F32)
    q = iota((nq, ndev), 0)
    peer = q >> 2 == iota((nq, ndev), 1)
    value = jnp.zeros((nq, 128), F32)
    for c in range(cap):
        column = jnp.broadcast_to(req[c : c + 1, :], (128, ndev)).T.astype(BF16)
        value = value + dot(onehot(peer & (q & (ROWS - 1) == c)), column)
    value = jnp.where(iota((nq, 128), 0) & (ROWS - 1) < cap, value, -1.0)
    value = value.astype(jnp.int32)
    for b in range(0, BLK_DEV, 128):
        g = onehot(value == iota((nq, 128), 1) + b)
        g_ref[:, b : b + 128] = g
        gt_ref[b : b + 128, :] = g.T

    for p in range(PARTS):

        def body(i, carry):
            each = FIRST_UNROLL // CHUNK
            for j in range(each):
                n = i * each + j
                copy(p, n).wait()
                n = n + DEPTH

                @pl.when(n < copies)
                def _():
                    copy(p, n).start()

                if p + 1 < PARTS:

                    @pl.when(n >= copies)
                    def _():
                        copy(p + 1, n - copies).start()

            for j in range(FIRST_UNROLL):
                turned[p][i * FIRST_UNROLL + j] = tiles[p][i * FIRST_UNROLL + j].T
            products(picked, tiles[p], res, i * FIRST_UNROLL, p * part, FIRST_UNROLL)
            return carry

        lax.fori_loop(0, part // FIRST_UNROLL, body, 0)
    sums = exact_dot(st_ref[...], res[...])
    send_ref[...] = with_scalar(sums, uu)


def ray_kernel(*refs):
    tiles, turned, refs = refs[:PARTS], refs[PARTS : 2 * PARTS], refs[2 * PARTS :]
    recv_ref, s_ref, st_ref, r_ref, rt_ref, uraw_ref, beta_ref = refs[:7]
    send_ref, uraw_out, alpha_ref, picked, res = refs[7:]
    part = tiles[0].shape[0]
    ntile = PARTS * part

    def run(parts):
        for p in range(PARTS):

            def body(i, carry):
                products(picked, parts[p], res, i * UNROLL, p * part, UNROLL)
                return carry

            lax.fori_loop(0, part // UNROLL, body, 0)

    got = dot(s_ref[...], recv_ref[...])
    picked[...] = got[:ntile].astype(BF16)
    alpha = jnp.sqrt(scalar_total(got[ntile : ntile + 1]))

    run(turned)
    product = exact_dot(rt_ref[...], res[...])
    beta = beta_ref[0:1, 0:1]
    uraw = product / alpha - alpha * (uraw_ref[...] / beta)
    uraw_out[...] = uraw
    alpha_ref[...] = jnp.broadcast_to(alpha, (8, 128))
    picked[...] = dot(r_ref[...], uraw.astype(BF16)).astype(BF16)
    uu = total(uraw * uraw)

    run(tiles)
    sums = exact_dot(st_ref[...], res[...])
    send_ref[...] = with_scalar(sums, uu)


def cell_kernel(first, last, *refs):
    recv_ref, gt_ref = refs[:2]
    recv = recv_ref[...]
    beta = jnp.sqrt(received_total(recv))
    grad = dot(gt_ref[...], recv)
    send_ref, vraw_out, beta_out = refs[-3:]
    vraw = grad / beta
    if not first:
        vraw_ref, alpha_ref = refs[3:5]
        vraw = vraw - beta * (vraw_ref[...] / alpha_ref[0:1, 0:1])
    vraw_out[...] = vraw
    beta_out[...] = jnp.broadcast_to(beta, (8, 128))
    vv = total(vraw * vraw)
    if last:
        send_ref[...] = jnp.broadcast_to(vv, send_ref.shape)
    else:
        send_ref[...] = with_scalar(dot(refs[2][...], vraw.astype(BF16)), vv)


def last_kernel(scale, *refs):
    recv_ref = refs[0]
    vraws = refs[1 : ITERS + 2]
    alphas = [ref[0:1, 0:1] for ref in refs[ITERS + 2 : 2 * ITERS + 2]]
    betas = [ref[0:1, 0:1] for ref in refs[2 * ITERS + 2 : 3 * ITERS + 3]]
    solution_ref, right_ref = refs[3 * ITERS + 3 :]
    vv = jnp.sum(jnp.sum(recv_ref[...], axis=0, keepdims=True)[:, 0:1], axis=1, keepdims=True)
    right_ref[...] = vraws[ITERS][...] * (scale / jnp.sqrt(vv))
    w = vraws[0][...] / alphas[0]
    phibar = betas[0]
    rhobar = alphas[0]
    solution = None
    for step in range(1, ITERS + 1):
        beta = betas[step]
        rhobar1 = jnp.sqrt(rhobar * rhobar + damping * damping)
        phibar = rhobar / rhobar1 * phibar
        rho = jnp.sqrt(rhobar1 * rhobar1 + beta * beta)
        cosine = rhobar1 / rho
        sine = beta / rho
        phi = cosine * phibar
        phibar = sine * phibar
        update = (phi / rho) * w
        solution = update if solution is None else solution + update
        if step < ITERS:
            alpha = alphas[step]
            w = vraws[step][...] / alpha - (sine * alpha / rho) * w
            rhobar = -cosine * alpha
    solution_ref[...] = solution


def shape(dims, dtype=F32):
    return jax.ShapeDtypeStruct(dims, dtype)


VMEM = pl.BlockSpec(memory_space=pltpu.VMEM)
SMEM = pl.BlockSpec(memory_space=pltpu.SMEM)
HBM = pl.BlockSpec(memory_space=pltpu.HBM)


def call(kernel, outs, in_specs, scratch=(), limit=8 << 20):
    if isinstance(in_specs, int):
        in_specs = [VMEM] * in_specs
    return pl.pallas_call(
        kernel,
        out_shape=outs,
        in_specs=in_specs,
        out_specs=[VMEM] * len(outs),
        scratch_shapes=list(scratch),
        compiler_params=pltpu.CompilerParams(vmem_limit_bytes=limit),
    )


def per_device(tiles, rays, tile_rows, tile_slots, tile_count, wanted):
    ndev = lax.axis_size(AXES)
    ntile, _, width = tiles.shape
    nrow = rays.shape[0]
    nq = ndev * ROWS
    cap = wanted.shape[2]

    def exchange(x):
        rows = x.shape[0] // ndev
        y = lax.all_to_all(
            x.reshape(ndev, rows, width), AXES, split_axis=0, concat_axis=0, tiled=True
        )
        return y.reshape(x.shape)

    def far(x):
        return pltpu.with_memory_space_constraint(x, pltpu.HBM)

    cells = shape((BLK_DEV, width))
    scalar = shape((8, width))
    sent = shape((nq, width), BF16)
    scratch = [
        pltpu.VMEM((ntile, width), BF16),
        pltpu.VMEM((ntile, width), F32),
    ]
    *kept, send, uraw, st, rt, s, r, g, gt = call(
        first_kernel,
        [
            *[shape((ntile // PARTS, width, width), BF16)] * (2 * PARTS),
            sent,
            shape((nrow, width)),
            shape((nq, ntile), BF16),
            shape((nrow, ntile), BF16),
            shape((ntile + EXTRA, nq), BF16),
            shape((ntile, nrow), BF16),
            shape((nq, BLK_DEV), BF16),
            shape((BLK_DEV, nq), BF16),
        ],
        [SMEM] + [HBM] * 5,
        [
            pltpu.VMEM((1, ntile), jnp.int32),
            pltpu.VMEM((1, ntile), jnp.int32),
            pltpu.VMEM((cap, ndev), jnp.int32),
            *scratch,
            pltpu.SemaphoreType.DMA((PARTS, ntile // PARTS // CHUNK)),
            pltpu.SemaphoreType.DMA((4,)),
        ],
    )(
        tile_count,
        far(tiles),
        far(rays),
        far(tile_rows.reshape(1, ntile)),
        far(tile_slots.reshape(1, ntile)),
        far(wanted[0].T),
    )

    vraws, alphas, betas = [], [], []
    for step in range(ITERS + 1):
        last = step == ITERS
        if step > 0:
            recv = exchange(send)
            send, uraw, alpha = call(
                ray_kernel,
                [sent, shape((nrow, width)), scalar],
                2 * PARTS + 7,
                scratch,
            )(*kept, recv, s, st, r, rt, uraw, betas[-1])
            alphas.append(alpha)
        recv = exchange(send)
        prior = [] if step == 0 else [vraws[-1], alphas[-1]]
        send, vraw, beta = call(
            functools.partial(cell_kernel, step == 0, last),
            [shape((ndev, width)) if last else sent, cells, scalar],
            3 + len(prior),
        )(recv, gt, g, *prior)
        vraws.append(vraw)
        betas.append(beta)
    recv = exchange(send)
    scale = float(BLK_DEV * width * ndev) ** 0.5
    return tuple(
        call(functools.partial(last_kernel, scale), [cells, cells], 3 * ITERS + 3)(
            recv, *vraws, *alphas, *betas
        )
    )


def solution(mesh):
    split = Mesh(mesh.devices.reshape(4, 4, 4, 2), AXES)
    placed = (
        P(AXES, None, None),
        P(AXES, None),
        P(AXES),
        P(AXES),
        P(AXES),
        P(AXES, None, None),
    )
    return jax.shard_map(
        per_device,
        mesh=split,
        in_specs=placed,
        out_specs=(P(AXES, None), P(AXES, None)),
        check_vma=False,
    )
```

time: 366 us -> 152 us (0.42); the launches traced: 359 us -> 152 us
  matrix products: 68.9 us -> 0 us
  other arithmetic: 37 us -> 0 us
  waiting for transfers between devices: 36.1 us -> 0 us
  blocking collectives: 157 us -> 121 us
  Pallas kernels: 0 us -> 30.1 us
  starting transfers between devices: 27.8 us -> 0 us
  between operations: 18.7 us -> 1.33 us
  local copies, waits for them, and re-layouts: 14.2 us -> 0 us
    psum x16 -> x0, blocking collectives: 129 us -> none  [over_axes(): value = lax.psum(value, axis)]
    all_to_all x2 -> x8, blocking collectives: 27.9 us -> 121 us  [exchange(): lax.all_to_all(x.reshape(ndev, rows, width), AXES, split_axis=0, concat_a...]
    dot_general x7 -> x0, matrix products: 68.9 us -> none  [the longest x3 36.6 us: per_device(): jnp.einsum('tij,tj->ti', tiles, forward_picked, preferred_element_type=jn...]
    all_to_all x5 -> x0, waiting for transfers between devices: 36.1 us -> none  [the longest x3 18.3 us: per_device(): lax.all_to_all(outgoing, SRC_REG, split_axis=0, concat_axis=0, tiled=True)]
    pallas_call x0 -> x9, Pallas kernels: none -> 30.1 us  [the longest x3 19.1 us: per_device(): call(ray_kernel, [sent, shape((nrow, width)), scalar], 2 * PARTS + 7, scr...]
    scatter-add x11 -> x0, other arithmetic: 27.8 us -> none  [the longest x3 12.3 us: per_device(): jax.ops.segment_sum(product, tile_rows, num_segments=row_blocks) / alpha]
    all_to_all x5 -> x0, starting transfers between devices: 27.8 us -> none  [the longest x2 16.1 us: per_device(): lax.all_to_all(slot_sums.astype(jnp.bfloat16), SRC_REG, split_axis=0, con...]
    gather x10 -> x0, local copies, waits for them, and re-layouts: 13.8 us -> none  [the longest x4 5.35 us: per_device(): picked = uraw.astype(jnp.bfloat16)[tile_rows]]
  transfers between devices with their start and end apart: 5 -> 0, of which waited for: 5 -> 0; matrix products, arithmetic and copies ran while one was open for 0% -> 0% of each run, Pallas kernels for 0% -> 0%
where the time goes in v2:
time: 152 us
  blocking collectives  121 us (80%)
  Pallas kernels  30.1 us (20%)
    all_to_all x8, blocking collectives, exchange(): lax.all_to_all(x.reshape(ndev, rows, width), AXES, split_axis=0, concat_a...  121 us
    pallas_call x3, Pallas kernels, per_device(): call(ray_kernel, [sent, shape((nrow, width)), scalar], 2 * PARTS + 7, scr...  19.1 us
    pallas_call x1, Pallas kernels, per_device(): call(first_kernel, [*[shape((ntile // PARTS, width, width), BF16)] * (2 *...  8.57 us

profile of v2, /device:TPU:1, one launch (start us, length us, event | category | flops | bytes accessed | tf_op | source)
XLA Modules:
  0.0 152.1 jit_solution(17998708137633025128)
XLA Ops:
  1.3 8.6 %shard_map.77 = (bf16[256,128,128]{2,1,0:T(8,128)(2,1)S(1)}, bf16[256,128,128]{2,1,0:T(8,128)(2,1)S(1)}, bf16[256,128,128]{2,1,0:T(8,128)(2,1)S(1)}, bf16[256,12...) custom-call(s32[1]{0:T(128)S(6)} %copy.9.count_ref, ...), custom_call_target="tpu_custom_call" | custom-call | tf_op jit(solution)/shard_map/pallas_call | solution.py:314
  9.9 21.3 %all_to_all.40 = bf16[128,4,128]{2,1,0:T(4,128)(2,1)S(1)} all-to-all(bf16[128,4,128]{2,1,0:T(4,128)(2,1)S(1)} %bitcast.31), channel_id=1, replica_groups=mesh['src_0'=4,'src_1'=4,'reg_0'=4,'reg_1'=2] {'src_0','src_1','reg_0','..., dimensions={0} | all-to-all | bytes 262144 | tf_op jit(solution)/shard_map/all_to_all | solution.py:299
  31.2 0.4 shard_map.78
  31.6 14.3 %all_to_all.41 = bf16[128,4,128]{2,1,0:T(4,128)(2,1)S(1)} all-to-all(bf16[128,4,128]{2,1,0:T(4,128)(2,1)S(1)} %bitcast.35), channel_id=1, replica_groups=mesh['src_0'=4,'src_1'=4,'reg_0'=4,'reg_1'=2] {'src_0','src_1','reg_0','..., dimensions={0} | all-to-all | bytes 262144 | tf_op jit(solution)/shard_map/all_to_all | solution.py:299
  45.9 6.4 %shard_map.79 = (bf16[512,128]{1,0:T(8,128)(2,1)S(1)}, f32[64,128]{1,0:T(8,128)S(1)}, f32[8,128]{1,0:T(8,128)S(1)}) custom-call(bf16[256,128,128]{2,1,0:T(8,128)(2,1)S(1)} %get-tuple-element.34.refs_0_, bf16[256,128,128]{2,1,0:T(8,128)(2,1)S(1)} %get-tuple-element.35.refs_1_, bf16[256,128,128]{2,1,0:T(8,128)(2,1)S(1)} %get-tuple-element.36.refs_2_, ...), custom_call_target="tpu_custom_call" | custom-call | tf_op jit(solution)/shard_map/pallas_call | solution.py:350
  52.3 14.3 %all_to_all.42 = bf16[128,4,128]{2,1,0:T(4,128)(2,1)S(1)} all-to-all(bf16[128,4,128]{2,1,0:T(4,128)(2,1)S(1)} %bitcast.33), channel_id=1, replica_groups=mesh['src_0'=4,'src_1'=4,'reg_0'=4,'reg_1'=2] {'src_0','src_1','reg_0','..., dimensions={0} | all-to-all | bytes 262144 | tf_op jit(solution)/shard_map/all_to_all | solution.py:299
  66.5 0.4 shard_map.80
  67.0 14.3 %all_to_all.43 = bf16[128,4,128]{2,1,0:T(4,128)(2,1)S(1)} all-to-all(bf16[128,4,128]{2,1,0:T(4,128)(2,1)S(1)} %bitcast.36), channel_id=1, replica_groups=mesh['src_0'=4,'src_1'=4,'reg_0'=4,'reg_1'=2] {'src_0','src_1','reg_0','..., dimensions={0} | all-to-all | bytes 262144 | tf_op jit(solution)/shard_map/all_to_all | solution.py:299
  81.2 6.4 %shard_map.81 = (bf16[512,128]{1,0:T(8,128)(2,1)S(1)}, f32[64,128]{1,0:T(8,128)S(1)}, f32[8,128]{1,0:T(8,128)S(1)}) custom-call(bf16[256,128,128]{2,1,0:T(8,128)(2,1)S(1)} %get-tuple-element.34.refs_0_, bf16[256,128,128]{2,1,0:T(8,128)(2,1)S(1)} %get-tuple-element.35.refs_1_, bf16[256,128,128]{2,1,0:T(8,128)(2,1)S(1)} %get-tuple-element.36.refs_2_, ...), custom_call_target="tpu_custom_call" | custom-call | tf_op jit(solution)/shard_map/pallas_call | solution.py:350
  87.6 14.3 %all_to_all.44 = bf16[128,4,128]{2,1,0:T(4,128)(2,1)S(1)} all-to-all(bf16[128,4,128]{2,1,0:T(4,128)(2,1)S(1)} %bitcast.34), channel_id=1, replica_groups=mesh['src_0'=4,'src_1'=4,'reg_0'=4,'reg_1'=2] {'src_0','src_1','reg_0','..., dimensions={0} | all-to-all | bytes 262144 | tf_op jit(solution)/shard_map/all_to_all | solution.py:299
  101.9 0.4 shard_map.82
  102.3 14.3 %all_to_all.45 = bf16[128,4,128]{2,1,0:T(4,128)(2,1)S(1)} all-to-all(bf16[128,4,128]{2,1,0:T(4,128)(2,1)S(1)} %bitcast.37), channel_id=1, replica_groups=mesh['src_0'=4,'src_1'=4,'reg_0'=4,'reg_1'=2] {'src_0','src_1','reg_0','..., dimensions={0} | all-to-all | bytes 262144 | tf_op jit(solution)/shard_map/all_to_all | solution.py:299
  116.6 6.4 %shard_map.83 = (bf16[512,128]{1,0:T(8,128)(2,1)S(1)}, f32[64,128]{1,0:T(8,128)}, f32[8,128]{1,0:T(8,128)S(1)}) custom-call(bf16[256,128,128]{2,1,0:T(8,128)(2,1)S(1)} %get-tuple-element.34.refs_0_, bf16[256,128,128]{2,1,0:T(8,128)(2,1)S(1)} %get-tuple-element.35.refs_1_, bf16[256,128,128]{2,1,0:T(8,128)(2,1)S(1)} %get-tuple-element.36.refs_2_, ...), custom_call_target="tpu_custom_call" | custom-call | tf_op jit(solution)/shard_map/pallas_call | solution.py:350
  123.0 14.3 %all_to_all.46 = bf16[128,4,128]{2,1,0:T(4,128)(2,1)S(1)} all-to-all(bf16[128,4,128]{2,1,0:T(4,128)(2,1)S(1)} %bitcast.32), channel_id=1, replica_groups=mesh['src_0'=4,'src_1'=4,'reg_0'=4,'reg_1'=2] {'src_0','src_1','reg_0','..., dimensions={0} | all-to-all | bytes 262144 | tf_op jit(solution)/shard_map/all_to_all | solution.py:299
  137.2 0.3 shard_map.84
  137.5 13.7 %all_to_all.47 = f32[128,1,128]{2,1,0:T(1,128)S(1)} all-to-all(f32[128,1,128]{2,1,0:T(1,128)S(1)} %bitcast.38), channel_id=1, replica_groups=mesh['src_0'=4,'src_1'=4,'reg_0'=4,'reg_1'=2] {'src_0','src_1','reg_0','..., dimensions={0} | all-to-all | bytes 131072 | tf_op jit(solution)/shard_map/all_to_all | solution.py:299
  151.3 0.8 shard_map.85

commit v3 on v2

--- a/solution.py
+++ b/solution.py
@@ -18,7 +18,7 @@
 ROWS = 4
 UNROLL = 128
 CHUNK = 32
-DEPTH = 4
+DEPTH = 6
 FIRST_UNROLL = 64
 PARTS = 2
 EXTRA = 16
@@ -131,53 +131,38 @@
     uraw = rays[...]
     picked[...] = dot(r_ref[...], uraw.astype(BF16)).astype(BF16)
     uu = total(uraw * uraw)
-    for q in range(0, nq, 128):
-        st = jnp.broadcast_to(slot_of, (128, ntile)) == iota((128, ntile), 0) + q
-        st = onehot(st)
-        st_ref[q : q + 128, :] = st
-        s_ref[:ntile, q : q + 128] = st.T
-    scalar = (iota((EXTRA, nq), 1) & (ROWS - 1) == 2) & (iota((EXTRA, nq), 0) == 0)
-    scalar = onehot(scalar)
-    s_ref[ntile:, :] = scalar
-    req = wanted[...].astype(F32)
-    q = iota((nq, ndev), 0)
-    peer = q >> 2 == iota((nq, ndev), 1)
-    value = jnp.zeros((nq, 128), F32)
-    for c in range(cap):
-        column = jnp.broadcast_to(req[c : c + 1, :], (128, ndev)).T.astype(BF16)
-        value = value + dot(onehot(peer & (q & (ROWS - 1) == c)), column)
-    value = jnp.where(iota((nq, 128), 0) & (ROWS - 1) < cap, value, -1.0)
-    value = value.astype(jnp.int32)
-    for b in range(0, BLK_DEV, 128):
-        g = onehot(value == iota((nq, 128), 1) + b)
-        g_ref[:, b : b + 128] = g
-        gt_ref[b : b + 128, :] = g.T
-
     for p in range(PARTS):
-
-        def body(i, carry):
-            each = FIRST_UNROLL // CHUNK
-            for j in range(each):
-                n = i * each + j
-                copy(p, n).wait()
-                n = n + DEPTH
-
-                @pl.when(n < copies)
-                def _():
-                    copy(p, n).start()
-
-                if p + 1 < PARTS:
-
-                    @pl.when(n >= copies)
-                    def _():
-                        copy(p + 1, n - copies).start()
-
-            for j in range(FIRST_UNROLL):
-                turned[p][i * FIRST_UNROLL + j] = tiles[p][i * FIRST_UNROLL + j].T
-            products(picked, tiles[p], res, i * FIRST_UNROLL, p * part, FIRST_UNROLL)
-            return carry
-
-        lax.fori_loop(0, part // FIRST_UNROLL, body, 0)
+        for i in range(0, part, FIRST_UNROLL):
+            for j in range(i // CHUNK, (i + FIRST_UNROLL) // CHUNK):
+                copy(p, j).wait()
+                n = p * copies + j + DEPTH
+                if n < PARTS * copies:
+                    copy(n // copies, n % copies).start()
+            for j in range(i, i + FIRST_UNROLL):
+                turned[p][j] = tiles[p][j].T
+            products(picked, tiles[p], res, i, p * part, FIRST_UNROLL)
+            if p == 0 and i == 0:
+                for q in range(0, nq, 128):
+                    st = jnp.broadcast_to(slot_of, (128, ntile)) == iota((128, ntile), 0) + q
+                    st = onehot(st)
+                    st_ref[q : q + 128, :] = st
+                    s_ref[:ntile, q : q + 128] = st.T
+                scalar = (iota((EXTRA, nq), 1) & (ROWS - 1) == 2) & (iota((EXTRA, nq), 0) == 0)
+                scalar = onehot(scalar)
+                s_ref[ntile:, :] = scalar
+                req = wanted[...].astype(F32)
+                q = iota((nq, ndev), 0)
+                peer = q >> 2 == iota((nq, ndev), 1)
+                value = jnp.zeros((nq, 128), F32)
+                for c in range(cap):
+                    column = jnp.broadcast_to(req[c : c + 1, :], (128, ndev)).T.astype(BF16)
+                    value = value + dot(onehot(peer & (q & (ROWS - 1) == c)), column)
+                value = jnp.where(iota((nq, 128), 0) & (ROWS - 1) < cap, value, -1.0)
+                value = value.astype(jnp.int32)
+                for b in range(0, BLK_DEV, 128):
+                    g = onehot(value == iota((nq, 128), 1) + b)
+                    g_ref[:, b : b + 128] = g
+                    gt_ref[b : b + 128, :] = g.T
     sums = exact_dot(st_ref[...], res[...])
     send_ref[...] = with_scalar(sums, uu)
 
@@ -191,12 +176,8 @@
 
     def run(parts):
         for p in range(PARTS):
-
-            def body(i, carry):
-                products(picked, parts[p], res, i * UNROLL, p * part, UNROLL)
-                return carry
-
-            lax.fori_loop(0, part // UNROLL, body, 0)
+            for i in range(0, part, UNROLL):
+                products(picked, parts[p], res, i, p * part, UNROLL)
 
     got = dot(s_ref[...], recv_ref[...])
     picked[...] = got[:ntile].astype(BF16)

time: 152 us -> 149 us (0.980)
  Pallas kernels: 30.1 us -> 26.8 us
    pallas_call x3, Pallas kernels: 19.1 us -> 16.3 us  [per_device(): call(ray_kernel, [sent, shape((nrow, width)), scalar], 2 * PARTS + 7, scr...]
where the time goes in v3:
time: 149 us
  blocking collectives  121 us (81%)
  Pallas kernels  26.8 us (18%)
    all_to_all x8, blocking collectives, exchange(): lax.all_to_all(x.reshape(ndev, rows, width), AXES, split_axis=0, concat_a...  121 us
    pallas_call x3, Pallas kernels, per_device(): call(ray_kernel, [sent, shape((nrow, width)), scalar], 2 * PARTS + 7, scr...  16.3 us
    pallas_call x1, Pallas kernels, per_device(): call(first_kernel, [*[shape((ntile // PARTS, width, width), BF16)] * (2 *...  8.08 us

profile of v3, /device:TPU:1, one launch (start us, length us, event | category | flops | bytes accessed | tf_op | source)
XLA Modules:
  0.0 148.8 jit_solution(9138118846978267998)
XLA Ops:
  1.3 8.1 %shard_map.77 = (bf16[256,128,128]{2,1,0:T(8,128)(2,1)S(1)}, bf16[256,128,128]{2,1,0:T(8,128)(2,1)S(1)}, bf16[256,128,128]{2,1,0:T(8,128)(2,1)S(1)}, bf16[256,12...) custom-call(s32[1]{0:T(128)S(6)} %copy.9.count_ref, ...), custom_call_target="tpu_custom_call" | custom-call | tf_op jit(solution)/shard_map/pallas_call | solution.py:295
  9.4 21.3 %all_to_all.40 = bf16[128,4,128]{2,1,0:T(4,128)(2,1)S(1)} all-to-all(bf16[128,4,128]{2,1,0:T(4,128)(2,1)S(1)} %bitcast.31), channel_id=1, replica_groups=mesh['src_0'=4,'src_1'=4,'reg_0'=4,'reg_1'=2] {'src_0','src_1','reg_0','..., dimensions={0} | all-to-all | bytes 262144 | tf_op jit(solution)/shard_map/all_to_all | solution.py:280
  30.7 0.4 shard_map.78
  31.1 14.3 %all_to_all.41 = bf16[128,4,128]{2,1,0:T(4,128)(2,1)S(1)} all-to-all(bf16[128,4,128]{2,1,0:T(4,128)(2,1)S(1)} %bitcast.35), channel_id=1, replica_groups=mesh['src_0'=4,'src_1'=4,'reg_0'=4,'reg_1'=2] {'src_0','src_1','reg_0','..., dimensions={0} | all-to-all | bytes 262144 | tf_op jit(solution)/shard_map/all_to_all | solution.py:280
  45.4 5.4 %shard_map.79 = (bf16[512,128]{1,0:T(8,128)(2,1)S(1)}, f32[64,128]{1,0:T(8,128)S(1)}, f32[8,128]{1,0:T(8,128)S(1)}) custom-call(bf16[256,128,128]{2,1,0:T(8,128)(2,1)S(1)} %get-tuple-element.34.refs_0_, bf16[256,128,128]{2,1,0:T(8,128)(2,1)S(1)} %get-tuple-element.35.refs_1_, bf16[256,128,128]{2,1,0:T(8,128)(2,1)S(1)} %get-tuple-element.36.refs_2_, ...), custom_call_target="tpu_custom_call" | custom-call | tf_op jit(solution)/shard_map/pallas_call | solution.py:331
  50.8 14.3 %all_to_all.42 = bf16[128,4,128]{2,1,0:T(4,128)(2,1)S(1)} all-to-all(bf16[128,4,128]{2,1,0:T(4,128)(2,1)S(1)} %bitcast.33), channel_id=1, replica_groups=mesh['src_0'=4,'src_1'=4,'reg_0'=4,'reg_1'=2] {'src_0','src_1','reg_0','..., dimensions={0} | all-to-all | bytes 262144 | tf_op jit(solution)/shard_map/all_to_all | solution.py:280
  65.1 0.4 shard_map.80
  65.5 14.3 %all_to_all.43 = bf16[128,4,128]{2,1,0:T(4,128)(2,1)S(1)} all-to-all(bf16[128,4,128]{2,1,0:T(4,128)(2,1)S(1)} %bitcast.36), channel_id=1, replica_groups=mesh['src_0'=4,'src_1'=4,'reg_0'=4,'reg_1'=2] {'src_0','src_1','reg_0','..., dimensions={0} | all-to-all | bytes 262144 | tf_op jit(solution)/shard_map/all_to_all | solution.py:280
  79.8 5.4 %shard_map.81 = (bf16[512,128]{1,0:T(8,128)(2,1)S(1)}, f32[64,128]{1,0:T(8,128)S(1)}, f32[8,128]{1,0:T(8,128)S(1)}) custom-call(bf16[256,128,128]{2,1,0:T(8,128)(2,1)S(1)} %get-tuple-element.34.refs_0_, bf16[256,128,128]{2,1,0:T(8,128)(2,1)S(1)} %get-tuple-element.35.refs_1_, bf16[256,128,128]{2,1,0:T(8,128)(2,1)S(1)} %get-tuple-element.36.refs_2_, ...), custom_call_target="tpu_custom_call" | custom-call | tf_op jit(solution)/shard_map/pallas_call | solution.py:331
  85.2 14.3 %all_to_all.44 = bf16[128,4,128]{2,1,0:T(4,128)(2,1)S(1)} all-to-all(bf16[128,4,128]{2,1,0:T(4,128)(2,1)S(1)} %bitcast.34), channel_id=1, replica_groups=mesh['src_0'=4,'src_1'=4,'reg_0'=4,'reg_1'=2] {'src_0','src_1','reg_0','..., dimensions={0} | all-to-all | bytes 262144 | tf_op jit(solution)/shard_map/all_to_all | solution.py:280
  99.5 0.4 shard_map.82
  99.9 14.3 %all_to_all.45 = bf16[128,4,128]{2,1,0:T(4,128)(2,1)S(1)} all-to-all(bf16[128,4,128]{2,1,0:T(4,128)(2,1)S(1)} %bitcast.37), channel_id=1, replica_groups=mesh['src_0'=4,'src_1'=4,'reg_0'=4,'reg_1'=2] {'src_0','src_1','reg_0','..., dimensions={0} | all-to-all | bytes 262144 | tf_op jit(solution)/shard_map/all_to_all | solution.py:280
  114.2 5.4 %shard_map.83 = (bf16[512,128]{1,0:T(8,128)(2,1)S(1)}, f32[64,128]{1,0:T(8,128)}, f32[8,128]{1,0:T(8,128)S(1)}) custom-call(bf16[256,128,128]{2,1,0:T(8,128)(2,1)S(1)} %get-tuple-element.34.refs_0_, bf16[256,128,128]{2,1,0:T(8,128)(2,1)S(1)} %get-tuple-element.35.refs_1_, bf16[256,128,128]{2,1,0:T(8,128)(2,1)S(1)} %get-tuple-element.36.refs_2_, ...), custom_call_target="tpu_custom_call" | custom-call | tf_op jit(solution)/shard_map/pallas_call | solution.py:331
  119.6 14.3 %all_to_all.46 = bf16[128,4,128]{2,1,0:T(4,128)(2,1)S(1)} all-to-all(bf16[128,4,128]{2,1,0:T(4,128)(2,1)S(1)} %bitcast.32), channel_id=1, replica_groups=mesh['src_0'=4,'src_1'=4,'reg_0'=4,'reg_1'=2] {'src_0','src_1','reg_0','..., dimensions={0} | all-to-all | bytes 262144 | tf_op jit(solution)/shard_map/all_to_all | solution.py:280
  133.9 0.3 shard_map.84
  134.2 13.7 %all_to_all.47 = f32[128,1,128]{2,1,0:T(1,128)S(1)} all-to-all(f32[128,1,128]{2,1,0:T(1,128)S(1)} %bitcast.38), channel_id=1, replica_groups=mesh['src_0'=4,'src_1'=4,'reg_0'=4,'reg_1'=2] {'src_0','src_1','reg_0','..., dimensions={0} | all-to-all | bytes 131072 | tf_op jit(solution)/shard_map/all_to_all | solution.py:280
  147.9 0.8 shard_map.85
